TPU v7x, 32 devices: a whole 2x2x4 slice. The times are simulated.
32 devices in a mesh: dp: 8 (over y, x, core), tensor: 4 (over z).
Axes of the slice: x: 2, y: 2, z: 4, core: 2. Of those that a mesh axis runs over, the one named last changes fastest.
Arguments:
- tokens: bfloat16 [128, 5376], P('dp'), may hold values from -6 to 6
- lengths: int32 [128], P('dp'), may hold values from 1 to 1024, as said below
- positions: int32 [128], P('dp'), may hold values from 1 to 33791, as said below
- in_gain: float32 [5376], replicated, may hold values from 0.25 to 1.75
- q_weight: bfloat16 [5376, 4096], P('dp', 'tensor'), may hold values from -0.078125 to 0.078125
- k_weight: bfloat16 [5376, 2048], P('dp', 'tensor'), may hold values from -0.078125 to 0.078125
- v_weight: bfloat16 [5376, 2048], P('dp', 'tensor'), may hold values from -0.078125 to 0.078125
- q_gain: float32 [128], replicated, may hold values from 0.1 to 1.9
- k_gain: float32 [128], replicated, may hold values from 0.1 to 1.9
- key_cache: bfloat16 [128, 1024, 2048], P('dp', None, 'tensor'), may hold values from -480 to 480
- value_cache: bfloat16 [128, 1024, 2048], P('dp', None, 'tensor'), may hold values from -6 to 6
- out_weight: bfloat16 [4096, 5376], P('tensor', 'dp'), may hold values from -0.09375 to 0.09375
- post_gain: float32 [5376], replicated, may hold values from 0.25 to 1.75
Outputs:
- hidden_out: bfloat16 [128, 5376], P('dp')
- new_keys: bfloat16 [128, 2048], P('dp', 'tensor')
- new_values: bfloat16 [128, 2048], P('dp', 'tensor')
Inputs may be any that keep to these rules, and one draw needn't show every extreme that they name: Slots 0 to lengths - 1 of a sequence hold its cache; some sequence has exactly 1024. `positions`: each position is at least the sequence's length.
All inputs are finite; a program needn't handle non-finite values.
Results may differ from a plain program's by a relative error of at most 0.012.
The roundings to bfloat16 on the way count: a program that leaves them out, or rounds other values in their place, can miss the bound.
Values may be sent and summed in bfloat16 or wider, within the bound.
A program may use at most 64 MiB of HBM per device.

v0:
```python
import jax
import jax.numpy as jnp
from jax import lax
from jax.sharding import PartitionSpec as P

HD = 128
QPRE = 168
epsilon = 1e-06
rope_base = 1000000.0
rope_factor = 8.0


def rms_scale(vectors, gain):
    mean_square = jnp.mean(vectors * vectors, axis=-1, keepdims=True)
    return vectors * lax.rsqrt(mean_square + epsilon) * gain


def rotate(vectors, positions):
    half_width = vectors.shape[-1] // 2
    exponent = jnp.arange(half_width, dtype=jnp.float32) * (2.0 / vectors.shape[-1])
    frequency = jnp.power(rope_base, -exponent)
    angles = (positions.astype(jnp.float32) / rope_factor)[:, None] * frequency[None, :]
    cos_part = jnp.cos(angles)[:, None, :]
    sin_part = jnp.sin(angles)[:, None, :]
    first_half = vectors[..., :half_width]
    second_half = vectors[..., half_width:]
    return jnp.concatenate(
        [
            first_half * cos_part - second_half * sin_part,
            second_half * cos_part + first_half * sin_part,
        ],
        axis=-1,
    )


def per_device(
    tokens,
    lengths,
    positions,
    in_gain,
    q_weight,
    k_weight,
    v_weight,
    q_gain,
    k_gain,
    key_cache,
    value_cache,
    out_weight,
    post_gain,
):
    tok_rows = tokens.shape[0]
    q_cols = q_weight.shape[1]
    kv_cols = k_weight.shape[1]
    local_heads = q_cols // HD
    local_kv = kv_cols // HD
    per_group = local_heads // local_kv
    cache_len = key_cache.shape[1]
    normed = rms_scale(tokens.astype(jnp.float32), in_gain).astype(jnp.bfloat16)
    spread = lax.all_to_all(normed, "dp", split_axis=1, concat_axis=0, tiled=True)
    joined = lax.psum_scatter(
        jnp.concatenate(
            [
                jnp.dot(spread, q_weight, preferred_element_type=jnp.float32),
                jnp.dot(spread, k_weight, preferred_element_type=jnp.float32),
                jnp.dot(spread, v_weight, preferred_element_type=jnp.float32),
            ],
            axis=1,
        ),
        "dp",
        scatter_dimension=0,
        tiled=True,
    )
    q_raw = joined[:, :q_cols]
    k_raw = joined[:, q_cols : q_cols + kv_cols]
    v_raw = joined[:, q_cols + kv_cols :]
    new_values = v_raw.astype(jnp.bfloat16)
    queries = (
        rotate(rms_scale(q_raw.reshape(tok_rows, local_heads, HD), q_gain), positions)
        * QPRE ** (-0.5)
    ).astype(jnp.bfloat16)
    new_keys = (
        rotate(rms_scale(k_raw.reshape(tok_rows, local_kv, HD), k_gain), positions)
        .astype(jnp.bfloat16)
        .reshape(tok_rows, kv_cols)
    )
    grouped = queries.reshape(tok_rows, local_kv, per_group, HD)
    cache_keys = key_cache.reshape(tok_rows, cache_len, local_kv, HD)
    cache_values = value_cache.reshape(tok_rows, cache_len, local_kv, HD)
    self_score = jnp.einsum(
        "bgrd,bgd->bgr",
        grouped,
        new_keys.reshape(tok_rows, local_kv, HD),
        preferred_element_type=jnp.float32,
    )
    self_values = new_values.reshape(tok_rows, local_kv, HD).astype(jnp.float32)
    scores = jnp.einsum("bgrd,bjgd->bgrj", grouped, cache_keys, preferred_element_type=jnp.float32)
    usable = jnp.arange(cache_len)[None, :] < lengths[:, None]
    scores = jnp.where(usable[:, None, None, :], scores, -jnp.inf)
    largest = jnp.maximum(jnp.max(scores, axis=-1), self_score)
    weights = jnp.exp(scores - largest[..., None])
    self_weight = jnp.exp(self_score - largest)
    running = jnp.sum(weights, axis=-1) + self_weight
    rounded_self = lax.optimization_barrier(self_weight.astype(jnp.bfloat16)).astype(jnp.float32)
    mixture = jnp.einsum(
        "bgrj,bjgd->bgrd",
        weights.astype(jnp.bfloat16),
        cache_values,
        preferred_element_type=jnp.float32,
    )
    mixture = mixture + rounded_self[..., None] * self_values[:, :, None, :]
    attended = (mixture / running[..., None]).reshape(tok_rows, q_cols).astype(jnp.bfloat16)
    products = jnp.dot(
        lax.all_gather(attended, "dp", axis=0, tiled=True),
        out_weight,
        preferred_element_type=jnp.float32,
    )
    partial_value = lax.all_to_all(products, "dp", split_axis=0, concat_axis=1, tiled=True)
    summed = lax.psum(partial_value, "tensor")
    hidden_out = (tokens.astype(jnp.float32) + rms_scale(summed, post_gain)).astype(jnp.bfloat16)
    return (hidden_out, new_keys, new_values)


def solution(mesh):
    return jax.shard_map(
        per_device,
        mesh=mesh,
        in_specs=(
            P("dp", None),
            P("dp"),
            P("dp"),
            P(),
            P("dp", "tensor"),
            P("dp", "tensor"),
            P("dp", "tensor"),
            P(),
            P(),
            P("dp", None, "tensor"),
            P("dp", None, "tensor"),
            P("tensor", "dp"),
            P(),
        ),
        out_specs=(P("dp", None), P("dp", "tensor"), P("dp", "tensor")),
        check_vma=False,
    )
```

profile of v0, /device:TPU:0, one launch (start us, length us, event | category | flops | bytes accessed | tf_op | source)
XLA Modules:
  0.0 155.1 jit_solution(9750821802335823185)
XLA Ops:
  7.2 1.2 fusion.18
  8.4 1.0 fusion.20
  9.8 11.2 %all_to_all.38 = bf16[16,8,672]{2,0,1:T(8,128)(2,1)S(1)} all-to-all(bf16[16,8,672]{2,0,1:T(8,128)(2,1)S(1)} %copy.23), channel_id=1, replica_groups=mesh['dp'=8,'tensor'=4] {'dp'}, dimensions={1} | all-to-all | bytes 344064 | tf_op jit(solution)/shard_map/all_to_all | solution.py:59
  21.4 1.4 fusion.33
  22.8 1.4 fusion.34
  24.2 1.1 pad_maximum_fusion
  25.3 0.7 convert_multiply_fusion.2
  26.0 0.7 iota_compare_fusion
  26.8 33.9 %reduce-scatter.2.cloned.1.call-done = f32[16,2048]{1,0:T(8,128)} async-done(((f32[128,2048]{1,0:T(8,128)}), f32[16,2048]{1,0:T(8,128)}) %reduce-scatter.2.cloned.1.call-update) | async-done | bytes 131088 | tf_op jit(solution)/shard_map/reduce_scatter | solution.py:60
  60.7 0.8 slice.32
  61.6 0.8 slice_bitcast_fusion
  62.6 0.7 multiply_multiply_fusion.1
  63.3 0.7 multiply_multiply_fusion
  64.7 11.0 %fusion.31 = (f32[16,4,2]{2,1,0:T(4,128)}, f32[16,4,2,1024]{3,2,1,0:T(2,128)S(1)}) fusion(bf16[16,4,2,128]{3,2,1,0:T(2,128)(2,1)S(1)} %fusion.26, pred[16,1024]{1,0:T(8,128)(4,1)S(1)} %iota_compare_fusion, bf16[16,1024,512]{2,1,0:T(8,128)(2,1)} %param.22), kind=kOutput, calls=%fused_computation.51 | convolution fusion | flops 33816448 | bytes 17351168 | tf_op jit(solution)/shard_map/bgrd,bjgd->bgrj/dot_general | solution.py:96
  75.7 0.8 fusion.30
  77.2 1.4 slice.46
  78.5 1.3 reshape.151
  80.4 7.3 %fusion.12 = bf16[16,4,2,128]{3,2,1,0:T(2,128)(2,1)S(1)} fusion(f32[16,4,2,1024]{3,2,1,0:T(2,128)S(1)} %get-tuple-element.12, f32[16,4,2]{2,1,0:T(4,128)S(1)} %get-tuple-element.4, f32[16,4,2]{2,1,0:T(4,128)S(1)} %bitcast.70, f32[16,4,128]{2,1,0:T(4,128)} %reshape.151, f32[16,4,2]{2,1,0:T(4,128)} %convert_element_type.58, bf16[16,1024,512]{2,1,0:T(8,128)(2,1)} %param.23), kind=kOutput, calls=%fused_computation.9 | convolution fusion | flops 33882112 | bytes 17368576 | tf_op jit(solution)/shard_map/bgrj,bjgd->bgrd/dot_general | solution.py:104
  87.7 9.2 %all_gather.3 = bf16[128,1024]{1,0:T(8,128)(2,1)S(1)} all-gather(bf16[16,1024]{1,0:T(8,128)(2,1)S(1)} %convert_element_type.62), channel_id=1, replica_groups=mesh['dp'=8,'tensor'=4] {'dp'}, dimensions={0}, use_global_device_ids=true | all-gather | bytes 294912 | tf_op jit(solution)/shard_map/all_gather | solution.py:113
  97.6 10.8 %all_to_all.39 = f32[8,16,672]{2,1,0:T(8,128)S(1)} all-to-all(f32[8,16,672]{2,1,0:T(8,128)S(1)} %bitcast.61), channel_id=1, replica_groups=mesh['dp'=8,'tensor'=4] {'dp'}, dimensions={0} | all-to-all | bytes 688128 | tf_op jit(solution)/shard_map/all_to_all | solution.py:117
  108.6 0.9 all_to_all.35
  110.3 35.1 %all-reduce.2.cloned.1.call-done = f32[16,5376]{1,0:T(8,128)} async-done(((f32[16,5376]{1,0:T(8,128)}), f32[16,5376]{1,0:T(8,128)}) %all-reduce.2.cloned.1.call-update) | async-done | bytes 344080 | tf_op jit(solution)/shard_map/psum | solution.py:118
  145.4 1.1 multiply_reduce_fusion
  146.5 1.8 %fusion.21 = bf16[16,5376]{1,0:T(8,128)(2,1)} fusion(bf16[16,5376]{1,0:T(8,128)(2,1)S(1)} %copy-done.1, f32[16,5376]{1,0:T(8,128)} %all-reduce.2.cloned.1.call-done, f32[5376]{0:T(1024)} %param.25, f32[16]{0:T(128)S(1)} %add_rsqrt_fusion.2), kind=kLoop, calls=%fused_computation.18 | loop fusion | flops 430080 | bytes 709696 | tf_op jit(solution)/shard_map/convert_element_type | solution.py:119
  (36 shorter events, 4.5 us)
Async XLA Ops:
  7.2 13.9 %copy-start = (bf16[672,1024]{1,0:T(8,128)(2,1)S(1)}, bf16[672,1024]{1,0:T(8,128)(2,1)}, u32[]{:S(2)}) copy-start(bf16[672,1024]{1,0:T(8,128)(2,1)} %param.17) | copy-start | bytes 4128772
  7.2 53.5 %reduce-scatter.2.cloned.1.call-start = ((), (), s32[]{:S(2)}) async-start(), calls=%async_computation.3 | async-start | bytes 1179648 | tf_op jit(solution)/shard_map/reduce_scatter | solution.py:60
  25.3 120.1 %all-reduce.2.cloned.1.call-start = ((), (), s32[]{:S(2)}) async-start(), calls=%async_computation.4 | async-start | bytes 688128 | tf_op jit(solution)/shard_map/psum | solution.py:118
  64.7 32.3 %copy-start.2 = (bf16[1024,672]{0,1:T(8,128)(2,1)S(1)}, bf16[1024,672]{0,1:T(8,128)(2,1)}, u32[]{:S(2)}) copy-start(bf16[1024,672]{0,1:T(8,128)(2,1)} %param.24) | copy-start | bytes 4128772
  75.7 70.8 %copy-start.1 = (bf16[16,5376]{1,0:T(8,128)(2,1)S(1)}, bf16[16,5376]{1,0:T(8,128)(2,1)}, u32[]{:S(2)}) copy-start(bf16[16,5376]{1,0:T(8,128)(2,1)} %param.13) | copy-start | bytes 516100
Sparse Core Ops, SparseCore 0:
  25.4 35.3 reduce-scatter.1
  109.7 35.6 all-reduce.1
where the time goes:
time: 156 us; the launch traced here: 155 us
  waiting for transfers between devices  69 us (44%)
  blocking collectives  31.3 us (20%)
  matrix products  22.2 us (14%)
  between operations  14.2 us (9%)
  other arithmetic  11.8 us (8%)
  local copies, waits for them, and re-layouts  6.5 us (4%)
    psum x1, waiting for transfers between devices, per_device(): summed = lax.psum(partial_value, 'tensor')  35.1 us
    reduce_scatter x1, waiting for transfers between devices, per_device(): lax.psum_scatter(jnp.concatenate([jnp.dot(spread, q_weight, preferred_ele...  33.9 us
    all_to_all x1, blocking collectives, per_device(): lax.all_to_all(normed, 'dp', split_axis=1, concat_axis=0, tiled=True)  11.2 us
    dot_general x1, matrix products, per_device(): jnp.einsum('bgrd,bjgd->bgrj', grouped, cache_keys, preferred_element_type...  11 us
    all_to_all x1, blocking collectives, per_device(): lax.all_to_all(products, 'dp', split_axis=0, concat_axis=1, tiled=True)  10.8 us
    all_gather x1, blocking collectives, per_device(): lax.all_gather(attended, 'dp', axis=0, tiled=True)  9.25 us
    dot_general x1, matrix products, per_device(): jnp.einsum('bgrj,bjgd->bgrd', weights.astype(jnp.bfloat16), cache_values,...  7.27 us
  transfers between devices with their start and end apart: 2, of which 2 were waited for; matrix products, arithmetic and copies ran while one was open for 1% of the time, Pallas kernels for 0%

commit v1 on v0

--- a/solution.py
+++ b/solution.py
@@ -114,7 +114,10 @@
         out_weight,
         preferred_element_type=jnp.float32,
     )
-    partial_value = lax.all_to_all(products, "dp", split_axis=0, concat_axis=1, tiled=True)
+    partial_value = jnp.concatenate(
+        lax.all_to_all(jnp.stack(jnp.split(products, lax.axis_size("dp"), axis=0)), "dp", 0, 0),
+        axis=1,
+    )
     summed = lax.psum(partial_value, "tensor")
     hidden_out = (tokens.astype(jnp.float32) + rms_scale(summed, post_gain)).astype(jnp.bfloat16)
     return (hidden_out, new_keys, new_values)

time: 156 us -> 159 us (1.019)
  local copies, waits for them, and re-layouts: 6.5 us -> 11.1 us
    another operation x0 -> x10, local copies, waits for them, and re-layouts: none -> 5.71 us  [per_device(): jnp.stack(jnp.split(products, lax.axis_size('dp'), axis=0))]
where the time goes in v1:
time: 159 us; the launch traced here: 158 us
  waiting for transfers between devices  69 us (43%)
  blocking collectives  31.3 us (20%)
  matrix products  22.1 us (14%)
  between operations  14.3 us (9%)
  local copies, waits for them, and re-layouts  11.1 us (7%)
  other arithmetic  10.5 us (7%)
    psum x1, waiting for transfers between devices, per_device(): summed = lax.psum(partial_value, 'tensor')  35.1 us
    reduce_scatter x1, waiting for transfers between devices, per_device(): lax.psum_scatter(jnp.concatenate([jnp.dot(spread, q_weight, preferred_ele...  33.9 us
    all_to_all x1, blocking collectives, per_device(): lax.all_to_all(normed, 'dp', split_axis=1, concat_axis=0, tiled=True)  11.2 us
    all_to_all x1, blocking collectives, per_device(): lax.all_to_all(jnp.stack(jnp.split(products, lax.axis_size('dp'), axis=0)...  10.8 us
    dot_general x1, matrix products, per_device(): jnp.einsum('bgrd,bjgd->bgrj', grouped, cache_keys, preferred_element_type...  10.4 us
    all_gather x1, blocking collectives, per_device(): lax.all_gather(attended, 'dp', axis=0, tiled=True)  9.27 us
    dot_general x1, matrix products, per_device(): jnp.einsum('bgrj,bjgd->bgrd', weights.astype(jnp.bfloat16), cache_values,...  7.87 us
    another operation x10, local copies, waits for them, and re-layouts, per_device(): jnp.stack(jnp.split(products, lax.axis_size('dp'), axis=0))  5.71 us
  transfers between devices with their start and end apart: 2, of which 2 were waited for; matrix products, arithmetic and copies ran while one was open for 1% of the time, Pallas kernels for 0%

profile of v1, /device:TPU:0, one launch (start us, length us, event | category | flops | bytes accessed | tf_op | source)
XLA Modules:
  0.0 158.3 jit_solution(11721423683232220746)
XLA Ops:
  7.2 1.2 fusion.18
  8.4 1.0 fusion.20
  9.8 11.2 %all_to_all.24 = bf16[16,8,672]{2,0,1:T(8,128)(2,1)S(1)} all-to-all(bf16[16,8,672]{2,0,1:T(8,128)(2,1)S(1)} %copy.34), channel_id=1, replica_groups=mesh['dp'=8,'tensor'=4] {'dp'}, dimensions={1} | all-to-all | bytes 344064 | tf_op jit(solution)/shard_map/all_to_all | solution.py:59
  21.0 1.4 fusion.34
  22.4 1.4 fusion.33
  24.2 1.1 pad_maximum_fusion
  26.8 33.9 %reduce-scatter.2.cloned.1.call-done = f32[16,2048]{1,0:T(8,128)} async-done(((f32[128,2048]{1,0:T(8,128)}), f32[16,2048]{1,0:T(8,128)}) %reduce-scatter.2.cloned.1.call-update) | async-done | bytes 131088 | tf_op jit(solution)/shard_map/reduce_scatter | solution.py:60
  60.7 0.8 slice.46
  61.5 0.8 slice_bitcast_fusion.8
  62.4 0.8 slice.32
  64.1 0.7 multiply_multiply_fusion.1
  65.5 10.4 %fusion.31 = (f32[16,4,2]{2,1,0:T(4,128)S(1)}, f32[16,4,2,1024]{3,2,1,0:T(2,128)S(1)}) fusion(bf16[16,4,2,128]{3,2,1,0:T(2,128)(2,1)S(1)} %fusion.26, pred[16,1024]{1,0:T(8,128)(4,1)S(1)} %iota_compare_fusion, bf16[16,1024,512]{2,1,0:T(8,128)(2,1)} %param.22), kind=kOutput, calls=%fused_computation.67 | convolution fusion | flops 33816448 | bytes 17351168 | tf_op jit(solution)/shard_map/bgrd,bjgd->bgrj/dot_general | solution.py:96
  76.5 7.9 %fusion.12 = bf16[16,4,2,128]{3,2,1,0:T(2,128)(2,1)} fusion(f32[16,4,2,1024]{3,2,1,0:T(2,128)S(1)} %get-tuple-element.20, f32[16,4,2]{2,1,0:T(4,128)S(1)} %get-tuple-element.4, f32[16,4,2]{2,1,0:T(4,128)S(1)} %bitcast.84, f32[16,4,128]{2,1,0:T(4,128)S(1)} %reshape.156, f32[16,4,2]{2,1,0:T(4,128)S(1)} %convert_element_type.58, bf16[16,1024,512]{2,1,0:T(8,128)(2,1)} %param.23), kind=kOutput, calls=%fused_computation.9 | convolution fusion | flops 33882112 | bytes 17368576 | tf_op jit(solution)/shard_map/bgrj,bjgd->bgrd/dot_general | solution.py:104
  84.4 0.8 convert_element_type.62
  85.2 9.3 %all_gather.3 = bf16[128,1024]{1,0:T(8,128)(2,1)S(1)} all-gather(bf16[16,1024]{1,0:T(8,128)(2,1)S(1)} %convert_element_type.62), channel_id=1, replica_groups=mesh['dp'=8,'tensor'=4] {'dp'}, dimensions={0}, use_global_device_ids=true | all-gather | bytes 294912 | tf_op jit(solution)/shard_map/all_gather | solution.py:113
  95.0 1.7 %slice_bitcast_fusion = (f32[1,16,672]{1,2,0:T(8,128)}, f32[1,16,672]{1,2,0:T(8,128)}, f32[1,16,672]{1,2,0:T(8,128)}, f32[1,16,672]{1,2,0:T(8,128)S(1)}, f32[1,1...) fusion(f32[128,672]{0,1:T(8,128)S(1)} %fusion.35), kind=kLoop, calls=%fused_computation.19 | loop fusion | bytes 688128 | tf_op jit(solution)/shard_map/stack | solution.py:118
  96.7 1.1 copy.44
  97.8 1.1 copy.43
  98.9 1.1 copy.42
  100.8 10.8 %all_to_all.25 = f32[8,16,672]{2,1,0:T(8,128)S(1)} all-to-all(f32[8,16,672]{2,1,0:T(8,128)S(1)} %constant_dynamic-update-slice_fusion), channel_id=1, replica_groups=mesh['dp'=8,'tensor'=4] {'dp'}, dimensions={0} | all-to-all | bytes 688128 | tf_op jit(solution)/shard_map/all_to_all | solution.py:118
  111.9 0.9 reshape.155
  113.5 35.1 %all-reduce.2.cloned.1.call-done = f32[16,5376]{1,0:T(8,128)} async-done(((f32[16,5376]{1,0:T(8,128)}), f32[16,5376]{1,0:T(8,128)}) %all-reduce.2.cloned.1.call-update) | async-done | bytes 344080 | tf_op jit(solution)/shard_map/psum | solution.py:121
  148.6 1.1 multiply_reduce_fusion
  149.7 1.8 %fusion.21 = bf16[16,5376]{1,0:T(8,128)(2,1)} fusion(bf16[16,5376]{1,0:T(8,128)(2,1)S(1)} %copy-done.1, f32[16,5376]{1,0:T(8,128)} %all-reduce.2.cloned.1.call-done, f32[5376]{0:T(1024)} %param.25, f32[16]{0:T(128)S(1)} %add_rsqrt_fusion.2), kind=kLoop, calls=%fused_computation.18 | loop fusion | flops 430080 | bytes 709696 | tf_op jit(solution)/shard_map/convert_element_type | solution.py:122
  (55 shorter events, 6.8 us)
Async XLA Ops:
  7.2 16.6 %copy-start = (bf16[672,1024]{1,0:T(8,128)(2,1)S(1)}, bf16[672,1024]{1,0:T(8,128)(2,1)}, u32[]{:S(2)}) copy-start(bf16[672,1024]{1,0:T(8,128)(2,1)} %param.17) | copy-start | bytes 4128772
  7.2 53.6 %reduce-scatter.2.cloned.1.call-start = ((), (), s32[]{:S(2)}) async-start(), calls=%async_computation.3 | async-start | bytes 1179648 | tf_op jit(solution)/shard_map/reduce_scatter | solution.py:60
  25.3 123.3 %all-reduce.2.cloned.1.call-start = ((), (), s32[]{:S(2)}) async-start(), calls=%async_computation.4 | async-start | bytes 688128 | tf_op jit(solution)/shard_map/psum | solution.py:121
  61.5 22.9 %copy-start.3 = (bf16[16,512]{1,0:T(8,128)(2,1)}, bf16[16,512]{1,0:T(8,128)(2,1)S(1)}, u32[]{:S(2)}) copy-start(bf16[16,512]{1,0:T(8,128)(2,1)S(1)} %slice.46) | copy-start | bytes 49156
  65.5 29.0 %copy-start.2 = (bf16[1024,672]{0,1:T(8,128)(2,1)S(1)}, bf16[1024,672]{0,1:T(8,128)(2,1)}, u32[]{:S(2)}) copy-start(bf16[1024,672]{0,1:T(8,128)(2,1)} %param.24) | copy-start | bytes 4128772
  76.5 73.2 %copy-start.1 = (bf16[16,5376]{1,0:T(8,128)(2,1)S(1)}, bf16[16,5376]{1,0:T(8,128)(2,1)}, u32[]{:S(2)}) copy-start(bf16[16,5376]{1,0:T(8,128)(2,1)} %param.13) | copy-start | bytes 516100
Sparse Core Ops, SparseCore 0:
  25.4 35.3 reduce-scatter.1
  112.9 35.6 all-reduce.1
